TPU v7x, 256 devices: a whole 4x4x8 slice. The times are simulated.
256 devices in a mesh: tp: 32 (over z, y), dp: 8 (over x, core).
Axes of the slice: x: 4, y: 4, z: 8, core: 2. Of those that a mesh axis runs over, the one named last changes fastest.
Arguments:
- a_mat: bfloat16 [4096, 32768], P(('dp', 'tp'))
- b_mat: bfloat16 [32768, 11008], P(('dp', 'tp'))
Outputs:
- output: bfloat16 [4096, 11008], P(('dp', 'tp'))
All inputs are finite; a program needn't handle non-finite values.
Results may differ from a plain program's by a relative error of at most 0.001.
Values are sent between devices in bfloat16 or wider.
A program may use at most 768 MiB of HBM per device.

v0:
```python
import jax
import jax.numpy as jnp
from jax import lax
from jax.sharding import PartitionSpec as P


def solution(mesh):
    spec_rows = P(("dp", "tp"), None)

    def local_block(a_rows, b_rows):
        a_cols = lax.all_to_all(a_rows, "dp", 1, 0, tiled=True)
        b_slab = lax.all_gather(b_rows, "tp", axis=0, tiled=True)
        part_prod = jnp.dot(a_cols, b_slab, preferred_element_type=jnp.float32)
        summed = lax.psum_scatter(part_prod, "dp", scatter_dimension=0, tiled=True)
        return summed.astype(jnp.bfloat16)

    return jax.shard_map(local_block, mesh=mesh, in_specs=(spec_rows, spec_rows), out_specs=spec_rows, check_vma=False)
```

profile of v0, /device:TPU:1, one launch (start us, length us, event | category | flops | bytes accessed | tf_op | source)
XLA Modules:
  0.0 661.0 jit_solution(13515890278413269847)
XLA Ops:
  6.5 0.0 all-gather.2.cloned.1.call-start
  6.5 0.7 all-gather.2.cloned.1.call-update
  7.3 0.0 reduce-scatter.2.cloned.1.call-start
  7.3 1.3 copy.7
  8.6 20.5 %all_to_all.19 = bf16[16,8,4096]{2,0,1:T(8,128)(2,1)S(1)} all-to-all(bf16[16,8,4096]{2,0,1:T(8,128)(2,1)S(1)} %bitcast.10), channel_id=1, replica_groups=mesh['tp'=32,'dp'=8] {'dp'}, dimensions={1} | all-to-all | bytes 2097152 | tf_op jit(solution)/shard_map/all_to_all | solution.py:11
  29.1 550.9 %all-gather.2.cloned.1.call-done = bf16[4096,11008]{1,0:T(8,128)(2,1)} async-done(((bf16[128,11008]{1,0:T(8,128)(2,1)}), bf16[4096,11008]{1,0:T(8,128)(2,1)}) %all-gather.2.cloned.1.call-update) | async-done | bytes 90177552 | tf_op jit(solution)/shard_map/all_gather | solution.py:12
  580.0 32.7 %fusion = f32[128,11008]{1,0:T(8,128)} fusion(bf16[128,4096]{1,0:T(8,128)(2,1)S(1)} %bitcast.9, bf16[4096,11008]{1,0:T(8,128)(2,1)} %all-gather.2.cloned.1.call-done), kind=kOutput, calls=%fused_computation.1 | convolution fusion | flops 11542724608 | bytes 96862208 | tf_op jit(solution)/shard_map/dot_general | solution.py:13
  612.8 0.0 reduce-scatter.2.cloned.1.call-update
  612.8 39.5 %reduce-scatter.2.cloned.1.call-done = f32[16,11008]{1,0:T(8,128)} async-done(((f32[128,11008]{1,0:T(8,128)}), f32[16,11008]{1,0:T(8,128)}) %reduce-scatter.2.cloned.1.call-update) | async-done | bytes 704528 | tf_op jit(solution)/shard_map/reduce_scatter | solution.py:14
  652.3 1.9 convert_element_type.3
Async XLA Ops:
  6.5 573.5 %all-gather.2.cloned.1.call-start = ((), (), s32[]{:S(2)}) async-start(), calls=%async_computation.2 | async-start | bytes 92995584 | tf_op jit(solution)/shard_map/all_gather | solution.py:12
  7.3 645.1 %reduce-scatter.2.cloned.1.call-start = ((), (), s32[]{:S(2)}) async-start(), calls=%async_computation.3 | async-start | bytes 6340608 | tf_op jit(solution)/shard_map/reduce_scatter | solution.py:14
Sparse Core Ops, SparseCore 0:
  9.9 570.0 all-gather.1
  612.9 39.3 reduce-scatter.1
where the time goes:
time: 662 us; the launch traced here: 661 us
  waiting for transfers between devices  591 us (89%)
  matrix products  32.7 us (5%)
  blocking collectives  20.5 us (3%)
  between operations  13.4 us (2%)
    all_gather x1, waiting for transfers between devices, local_block(): b_slab = lax.all_gather(b_rows, 'tp', axis=0, tiled=True)  551 us
    reduce_scatter x1, waiting for transfers between devices, local_block(): summed = lax.psum_scatter(part_prod, 'dp', scatter_dimension=0, tiled=True)  39.5 us
    dot_general x1, matrix products, local_block(): part_prod = jnp.dot(a_cols, b_slab, preferred_element_type=jnp.float32)  32.7 us
    all_to_all x1, blocking collectives, local_block(): a_cols = lax.all_to_all(a_rows, 'dp', 1, 0, tiled=True)  20.5 us
  transfers between devices with their start and end apart: 2, of which 2 were waited for; matrix products, arithmetic and copies ran while one was open for 0% of the time, Pallas kernels for 0%

commit v1 on v0

v1 whole, which is shorter than its diff:
```python
import functools

import jax
import jax.numpy as jnp
from jax import lax
from jax.experimental import pallas as pl
from jax.experimental.pallas import tpu as pltpu
from jax.sharding import PartitionSpec as P

MESH = pl.DeviceIdType.MESH

X, Y, Z = 4, 4, 8
KB = 128
RB = 16
K = X * Y * KB
M = X * Z * 2 * RB
NS = 22 * 128
W = 256
NCH = NS // W
STARTS = (0, 21, 43, 64)
HALF = Z * X * RB
BLK = X * RB

LX, LR, LD, LF = 5, 3, 2, 1

PEERS = [(0, 0), (0, 1), (1, 0), (7, 0), (1, 1), (7, 1), (2, 0), (6, 0), (2, 1), (6, 1),
         (3, 0), (5, 0), (3, 1), (5, 1), (4, 0), (4, 1)]
GROUPS = [PEERS[0:6], PEERS[6:10], PEERS[10:14], PEERS[14:16]]


def kernel(a_ref, b_ref, o_ref, af, bf, part, rcv, zr, relay, cs, cst,
           az, ax, aw, yo, yow, xd, xr, xf, yd, yf, cr, zs, cx, loc,
           s_x, s_y, s_yo, s_az, s_ax, s_c, s_o):
    dp, tp = lax.axis_index("dp"), lax.axis_index("tp")
    x, c = lax.div(dp, 2), lax.rem(dp, 2)
    z, y = lax.div(tp, Y), lax.rem(tp, Y)
    xp, xm, xo = lax.rem(x + 1, X), lax.rem(x + 3, X), lax.rem(x + 2, X)
    yp, ym = lax.rem(y + 1, Y), lax.rem(y + 3, Y)
    zp, zm = lax.rem(z + 1, Z), lax.rem(z + 7, Z)
    cc = 1 - c

    def dev(dx, dy, dz, dc):
        return {"dp": dx * 2 + dc, "tp": dz * Y + dy}

    def send(src, dst, s_sem, r_sem, to):
        pltpu.make_async_remote_copy(src_ref=src, dst_ref=dst, send_sem=s_sem, recv_sem=r_sem,
                                     device_id=to, device_id_type=MESH).start()

    def take(like, sem):
        pltpu.make_async_copy(like, like, sem).wait()

    to_xp, to_xm, to_xo = dev(xp, y, z, c), dev(xm, y, z, c), dev(xo, y, z, c)
    to_yp, to_ym = dev(x, yp, z, c), dev(x, ym, z, c)
    to_zp, to_zm = dev(x, y, zp, c), dev(x, y, zm, c)
    to_core = dev(x, y, z, cc)

    def peer(dz, dc, sign):
        return lax.rem(z + (dz if sign > 0 else Z - dz), Z), lax.rem(c + dc, 2)

    barrier = pltpu.get_barrier_semaphore()
    for to in (to_xp, to_xm, to_xo, to_yp, to_ym):
        pl.semaphore_signal(barrier, inc=1, device_id=to, device_id_type=MESH)
    for dz, dc in PEERS[1:]:
        pz, pc = peer(dz, dc, 1)
        pl.semaphore_signal(barrier, inc=1, device_id=dev(x, y, pz, pc), device_id_type=MESH)
    pl.semaphore_wait(barrier, 5 + len(PEERS) - 1)

    def start(sx):
        return (21 * sx + lax.div(sx, 2)) * 128

    def bcols(sx, j):
        return pl.ds(pl.multiple_of(start(sx) + j * W, 128), W)

    def cols(j):
        return pl.ds(pl.multiple_of(j * W, W), W)

    def krows(sx, sy, off=0, n=KB):
        return pl.ds(pl.multiple_of((sx * Y + sy) * KB + off, 64), n)

    def arows(sc, sz, sx):
        return pl.ds(pl.multiple_of(((sc * Z + sz) * X + sx) * RB, RB), RB)

    own_cols = pl.ds(pl.multiple_of(start(x), 128), NS)

    own_b = b_ref.at[:, own_cols]
    own_dst = bf.at[krows(x, y), :]
    send(own_b, own_dst, s_yo, yo.at[0], to_yp)
    send(own_b, own_dst, s_yo, yo.at[1], to_ym)
    pltpu.make_async_copy(own_b, own_dst, loc.at[0]).start()

    def xsend(j):
        full = bf.at[krows(x, y), cols(j)]
        send(b_ref.at[:, bcols(xp, j)], full, s_x.at[j], xd.at[0, j], to_xp)
        send(b_ref.at[:, bcols(xm, j)], full, s_x.at[j], xd.at[1, j], to_xm)
        send(b_ref.at[0:64, bcols(xo, j)], relay.at[0, :, cols(j)], s_x.at[j], xr.at[0, j], to_xp)
        send(b_ref.at[64:128, bcols(xo, j)], relay.at[1, :, cols(j)], s_x.at[j], xr.at[1, j], to_xm)

    def xrelay(j):
        r0, r1 = relay.at[0, :, cols(j)], relay.at[1, :, cols(j)]
        take(r0, xr.at[0, j])
        send(r0, bf.at[krows(xm, y, 0, 64), cols(j)], s_x.at[j], xf.at[0, j], to_xp)
        take(r1, xr.at[1, j])
        send(r1, bf.at[krows(xp, y, 64, 64), cols(j)], s_x.at[j], xf.at[1, j], to_xm)

    def ydirect(j):
        take(bf.at[krows(xm, y), cols(j)], xd.at[0, j])
        take(bf.at[krows(xp, y), cols(j)], xd.at[1, j])
        take(bf.at[krows(xo, y, 0, 64), cols(j)], xf.at[0, j])
        take(bf.at[krows(xo, y, 64, 64), cols(j)], xf.at[1, j])
        for sx in (xm, xp, xo):
            blk = bf.at[krows(sx, y), cols(j)]
            send(blk, blk, s_y.at[j], yd.at[0, j], to_yp)
            send(blk, blk, s_y.at[j], yd.at[1, j], to_ym)

    def yforward(j):
        take(bf.at[0:3 * KB, cols(j)], yd.at[0, j])
        for sx in (xm, xp, xo):
            blk = bf.at[krows(sx, ym, 0, 64), cols(j)]
            send(blk, blk, s_y.at[j], yf.at[0, j], to_yp)
        take(bf.at[0:3 * KB, cols(j)], yd.at[1, j])
        for sx in (xm, xp, xo):
            blk = bf.at[krows(sx, yp, 64, 64), cols(j)]
            send(blk, blk, s_y.at[j], yf.at[1, j], to_ym)

    def yforward_own():
        take(own_dst, yo.at[0])
        blk = bf.at[krows(x, ym, 0, 64), :]
        send(blk, blk, s_yo, yow.at[0], to_yp)
        take(own_dst, yo.at[1])
        blk = bf.at[krows(x, yp, 64, 64), :]
        send(blk, blk, s_yo, yow.at[1], to_ym)

    def a_seg(sx, sc, sz):
        return a_ref.at[:, pl.ds(pl.multiple_of(((sx * 2 + sc) * Z * Y + sz * Y) * KB, Y * KB), Y * KB)]

    def a_send():
        mine = arows(c, z, x)
        for sx in range(X):
            dst = af.at[mine, sx * Y * KB:(sx + 1) * Y * KB]
            pltpu.make_async_copy(a_seg(sx, c, z), dst, loc.at[1]).start()
        for dz, dc in PEERS[1:]:
            pz, pc = peer(dz, dc, 1)
            for sx in range(X):
                dst = af.at[mine, sx * Y * KB:(sx + 1) * Y * KB]
                send(a_seg(sx, pc, pz), dst, s_az, az.at[c * Z + z], dev(x, y, pz, pc))

    def a_direct(g):
        for dz, dc in GROUPS[g]:
            sz, sc = peer(dz, dc, -1)
            blk = af.at[arows(sc, sz, x), :]
            take(blk, loc.at[1] if (dz, dc) == (0, 0) else az.at[sc * Z + sz])
            send(blk, blk, s_ax, ax.at[0, g], to_xp)
            send(blk, blk, s_ax, ax.at[1, g], to_xm)

    def a_forward(g):
        n = len(GROUPS[g]) * RB
        take(af.at[0:n, :], ax.at[0, g])
        for dz, dc in GROUPS[g]:
            sz, sc = peer(dz, dc, -1)
            blk = af.at[arows(sc, sz, xm), 0:K // 2]
            send(blk, blk, s_ax, aw.at[0], to_xp)
        take(af.at[0:n, :], ax.at[1, g])
        for dz, dc in GROUPS[g]:
            sz, sc = peer(dz, dc, -1)
            blk = af.at[arows(sc, sz, xp), K // 2:K]
            send(blk, blk, s_ax, aw.at[1], to_xm)

    mine = pl.multiple_of(c * HALF, HALF)
    other = pl.multiple_of(cc * HALF, HALF)

    def first(j):
        take(own_dst, loc.at[0])
        for d in range(2):
            take(bf.at[0:64, :], yow.at[d])
            take(af.at[0:16 * RB, 0:K // 2], aw.at[d])

    def matmul(j):
        for d in range(2):
            take(bf.at[0:3 * 64, cols(j)], yf.at[d, j])
        part[j] = jnp.dot(af[...], bf[:, cols(j)], preferred_element_type=jnp.float32)
        send(part.at[j, pl.ds(other, HALF), :], rcv.at[j], s_c.at[j], cr.at[j], to_core)

    def zrows(k):
        b = lax.rem(z + k, Z)
        return (pl.ds(pl.multiple_of(mine + b * BLK, BLK), BLK),
                pl.ds(pl.multiple_of(b * BLK, BLK), BLK))

    def zstep1(j):
        take(rcv.at[j], cr.at[j])

        def add(k, carry):
            p, r = zrows(k)
            part[j, p, :] += rcv[j, r, :]
            return carry

        add(4, 0)
        p, _ = zrows(4)
        send(part.at[j, p, 0:128], zr.at[j, 0, 0, :, 0:128], s_c.at[j], zs.at[0, j], to_zp)
        send(part.at[j, p, 128:256], zr.at[j, 1, 0, :, 128:256], s_c.at[j], zs.at[4, j], to_zm)
        lax.fori_loop(0, 4, add, 0)
        lax.fori_loop(5, 8, add, 0)

    def zstep(j, s):
        for d in range(2):
            p, _ = zrows((5 - s) if d == 0 else (3 + s))
            got = zr.at[j, d, s - 2]
            if s == 2:
                half = slice(0, 128) if d == 0 else slice(128, 256)
                take(zr.at[j, d, 0, :, half], zs.at[4 * d, j])
                part[j, p, half] += zr[j, d, 0, :, half]
            else:
                take(got, zs.at[4 * d + s - 2, j])
                part[j, p, :] += got[...]
            send(part.at[j, p, :], zr.at[j, d, s - 1], s_c.at[j], zs.at[4 * d + s - 1, j],
                 to_zp if d == 0 else to_zm)

    def finish(j):
        p, _ = zrows(0)
        for d in range(2):
            take(zr.at[j, d, 3], zs.at[4 * d + 3, j])
        cs[j] = (part[j, p, :] + zr[j, 0, 3] + zr[j, 1, 3]).astype(jnp.bfloat16)
        for sx, to in ((xp, to_xp), (xm, to_xm), (xo, to_xo)):
            rows = pl.ds(pl.multiple_of(sx * RB, RB), RB)
            send(cs.at[j, rows, :], cst.at[x, :, cols(j)], s_o.at[j], cx.at[j], to)
        rows = pl.ds(pl.multiple_of(x * RB, RB), RB)
        cst[x, :, cols(j)] = cs[j, rows, :]

    for j in range(4):
        xsend(j)
    a_send()
    for j in range(LR):
        xrelay(j)
    a_direct(0)
    for j in range(LD):
        ydirect(j)
    a_direct(1)
    yforward_own()
    a_direct(2)
    a_direct(3)
    for j in range(4, LX):
        xsend(j)
    for g in range(len(GROUPS)):
        a_forward(g)
    for j in range(LF):
        yforward(j)

    def body(i, carry):
        def at(off, fn):
            j = i + off
            lo, hi = max(0, -off), NCH - off

            @pl.when(jnp.logical_and(i >= lo, i < hi))
            def _():
                fn(j)

        at(LX, xsend)
        at(LR, xrelay)
        at(LD, ydirect)
        at(LF, yforward)

        @pl.when(i == 0)
        def _():
            first(0)

        at(0, matmul)
        at(-5, finish)
        at(-4, lambda j: zstep(j, 4))
        at(-3, lambda j: zstep(j, 3))
        at(-2, lambda j: zstep(j, 2))
        at(-1, zstep1)
        return carry

    lax.fori_loop(0, NCH + 5, body, 0)

    def drain(j, carry):
        take(cst.at[0:3, :, 0:W], cx.at[j])
        return carry

    lax.fori_loop(0, NCH, drain, 0)
    outs = []
    for sx in range(X):
        lo = STARTS[sx] * 128 + (128 if sx in (1, 3) else 0)
        hi = 11008 if sx == X - 1 else STARTS[sx] * 128 + NS
        off = lo - STARTS[sx] * 128
        cp = pltpu.make_async_copy(cst.at[sx, :, off:off + hi - lo], o_ref.at[:, lo:hi], loc.at[2 + sx])
        cp.start()
        outs.append(cp)

    def sent(j, carry):
        take(part.at[0, 0:256, :], s_x.at[j])
        take(part.at[0, 0:576, :], s_y.at[j])
        take(part.at[0, 0:960, :], s_c.at[j])
        take(part.at[0, 0:24, :], s_o.at[j])
        return carry

    lax.fori_loop(0, NCH, sent, 0)
    take(part.at[0:3, 0:704, :], s_yo)
    take(part.at[0, 0:960, :], s_az)
    take(part.at[0:3], s_ax)
    for cp in outs:
        cp.wait()


def solution(mesh):
    spec_rows = P(("dp", "tp"), None)
    dma = pltpu.SemaphoreType.DMA

    call = pl.pallas_call(
        kernel,
        out_shape=jax.ShapeDtypeStruct((RB, 11008), jnp.bfloat16),
        in_specs=[pl.BlockSpec(memory_space=pl.ANY)] * 2,
        out_specs=pl.BlockSpec(memory_space=pl.ANY),
        scratch_shapes=[
            pltpu.VMEM((M, K), jnp.bfloat16),
            pltpu.VMEM((K, NS), jnp.bfloat16),
            pltpu.VMEM((NCH, M, W), jnp.float32),
            pltpu.VMEM((NCH, HALF, W), jnp.float32),
            pltpu.VMEM((NCH, 2, 4, BLK, W), jnp.float32),
            pltpu.VMEM((2, 64, NS), jnp.bfloat16),
            pltpu.VMEM((NCH, BLK, W), jnp.bfloat16),
            pltpu.VMEM((X, RB, NS), jnp.bfloat16),
            dma((16,)), dma((2, 4)), dma((2,)), dma((2,)), dma((2,)),
            dma((2, NCH)), dma((2, NCH)), dma((2, NCH)), dma((2, NCH)), dma((2, NCH)),
            dma((NCH,)), dma((8, NCH)), dma((NCH,)), dma((6,)),
            dma((NCH,)), dma((NCH,)), dma, dma, dma, dma((NCH,)), dma((NCH,)),
        ],
        compiler_params=pltpu.CompilerParams(
            collective_id=0, has_side_effects=True, vmem_limit_bytes=60 * 1024 * 1024),
    )

    return jax.shard_map(call, mesh=mesh, in_specs=(spec_rows, spec_rows), out_specs=spec_rows, check_vma=False)
```

time: 662 us -> 153 us (0.23)
  the two profiles are of different devices: /device:TPU:1 before, /device:TPU:32 now
where the time goes in v1:
time: 153 us
  Pallas kernels  151 us (99%)
  local copies, waits for them, and re-layouts  1.74 us (1%)
    pallas_call x1, Pallas kernels  151 us

profile of v1, /device:TPU:32, one launch (start us, length us, event | category | flops | bytes accessed | tf_op | source)
XLA Modules:
  0.0 152.7 jit_solution(12177292774657833318)
XLA Ops:
  0.0 151.0 %shard_map.28 = bf16[16,11008]{1,0:T(8,128)(2,1)} custom-call(bf16[16,32768]{1,0:T(8,128)(2,1)} %a_ref.1, bf16[128,11008]{1,0:T(8,128)(2,1)} %b_ref.1), custom_call_target="tpu_custom_call" | custom-call | tf_op jit(solution)/shard_map/pallas_call
  151.0 1.7 %copy.4 = bf16[16,11008]{1,0:T(8,128)(2,1)} copy(bf16[16,11008]{1,0:T(8,128)(2,1)} %shard_map.28) | data formatting | bytes 704512

commit v2 on v0

v2 whole, which is shorter than its diff:
```python
import jax
import jax.numpy as jnp
from jax import lax
from jax.experimental import pallas as pl
from jax.experimental.pallas import tpu as pltpu
from jax.sharding import PartitionSpec as P

MESH = pl.DeviceIdType.MESH

X, Y, Z = 4, 4, 8
KB = 128
RB = 16
K = X * Y * KB
NS = 22 * 128
BLK = X * RB

WIDTHS = [128] + [256] * 10 + [128]
CH = [(sum(WIDTHS[:j]), w) for j, w in enumerate(WIDTHS)]
NCH = len(CH)

REL = (4, 3, 5, 2, 6, 1, 7, 0)
GROUPS = ((0, 1), (1, 3), (3, 5), (5, 7), (7, 8))
PHASED = 6

ORDER = (
    ("yo",), ("x", 0), ("as",), ("x", 1), ("x", 2), ("ad", 0), ("yd", 0), ("yd", 1), ("x", 3), ("af", 0),
    ("yfo",), ("ad", 1), ("yf", 0), ("x", 4), ("ad", 2), ("yf", 1), ("x", 5), ("yd", 2), ("af", 1), ("mm", 0, 0),
    ("yd", 3), ("z", 0, 0), ("x", 6), ("mm", 1, 0), ("z", 1, 0), ("af", 2), ("yd", 4), ("yf", 2), ("ad", 3),
    ("mm", 0, 1), ("mm", 1, 1), ("yf", 3), ("z", 0, 1), ("z", 1, 1), ("x", 7), ("yd", 5), ("mm", 0, 2),
    ("yf", 4), ("mm", 1, 2), ("x", 8), ("z", 0, 2), ("mm", 2, 2), ("z", 1, 2), ("mm", 2, 1), ("mm", 2, 0),
    ("ad", 4), ("mm", 3, 2), ("mm", 3, 1), ("yd", 6), ("z", 2, 0), ("mm", 3, 0), ("x", 9), ("z", 3, 0),
    ("yf", 5), ("z", 2, 1), ("af", 3), ("mm", 4, 2), ("z", 3, 1), ("mm", 4, 1), ("yd", 7), ("mm", 4, 0),
    ("x", 10), ("z", 2, 2), ("z", 4, 0), ("yf", 6), ("z", 3, 2), ("af", 4), ("mm", 5, 2), ("mm", 5, 1),
    ("yd", 8), ("z", 4, 1), ("mm", 5, 0), ("x", 11), ("mm", 0, 3), ("mm", 1, 3), ("z", 5, 0), ("mm", 2, 3),
    ("yf", 7), ("z", 0, 3), ("mm", 3, 3), ("z", 1, 3), ("z", 4, 2), ("z", 2, 3), ("mm", 4, 3), ("mm", 5, 3),
    ("z", 3, 3), ("yd", 9), ("z", 5, 1), ("mm", 0, 4), ("mm", 1, 4), ("mm", 2, 4), ("mm", 3, 4), ("mm", 4, 4),
    ("mm", 5, 4), ("fin", 0), ("fin", 1), ("mm", 6, -1), ("yf", 8), ("z", 4, 3), ("fin", 2), ("mm", 7, -1),
    ("yd", 10), ("fin", 3), ("z", 6, 0), ("z", 5, 2), ("z", 7, 0), ("fin", 4), ("yf", 9), ("z", 6, 1),
    ("mm", 8, -1), ("yd", 11), ("z", 5, 3), ("z", 7, 1), ("z", 6, 2), ("z", 8, 0), ("yf", 10), ("fin", 5),
    ("mm", 9, -1), ("z", 7, 2), ("yf", 11), ("z", 6, 3), ("z", 8, 1), ("z", 9, 0), ("mm", 10, -1), ("z", 7, 3),
    ("mm", 11, -1), ("fin", 6), ("z", 10, 0), ("z", 8, 2), ("z", 11, 0), ("z", 9, 1), ("fin", 7), ("z", 10, 1),
    ("z", 8, 3), ("z", 11, 1), ("z", 9, 2), ("z", 10, 2), ("fin", 8), ("z", 11, 2), ("z", 9, 3), ("z", 10, 3),
    ("z", 11, 3), ("fin", 9), ("fin", 10), ("fin", 11),
)


def kernel(a_ref, b_ref, o_ref, af, bf, part, rcv, zr, cs,
           az, ax, aw, yo, yow, xd, yd, yf, cr, zs, cx, loc,
           s_x, s_y, s_yo, s_az, s_ax, s_c, s_o):
    dp, tp = lax.axis_index("dp"), lax.axis_index("tp")
    x, c = lax.div(dp, 2), lax.rem(dp, 2)
    z, y = lax.div(tp, Y), lax.rem(tp, Y)
    xp, xm, xo = lax.rem(x + 1, X), lax.rem(x + 3, X), lax.rem(x + 2, X)
    yp, ym = lax.rem(y + 1, Y), lax.rem(y + 3, Y)
    zp, zm = lax.rem(z + 1, Z), lax.rem(z + 7, Z)
    cc = 1 - c

    def dev(dx, dy, dz, dc):
        return {"dp": dx * 2 + dc, "tp": dz * Y + dy}

    def send(src, dst, s_sem, r_sem, to):
        pltpu.make_async_remote_copy(src_ref=src, dst_ref=dst, send_sem=s_sem, recv_sem=r_sem,
                                     device_id=to, device_id_type=MESH).start()

    def take(like, sem):
        pltpu.make_async_copy(like, like, sem).wait()

    to_xp, to_xm, to_xo = dev(xp, y, z, c), dev(xm, y, z, c), dev(xo, y, z, c)
    to_yp, to_ym = dev(x, yp, z, c), dev(x, ym, z, c)
    to_zp, to_zm = dev(x, y, zp, c), dev(x, y, zm, c)
    to_core = dev(x, y, z, cc)
    x_peers = ((xp, to_xp), (xm, to_xm), (xo, to_xo))

    def ahead(dz):
        return lax.rem(z + dz, Z)

    z_peers = [(dz, dc) for r in REL for dz in ((Z - r) % Z,) for dc in (0, 1) if dz or dc]

    def z_peer(dz, dc):
        return dev(x, y, ahead(dz), lax.rem(c + dc, 2))

    barrier = pltpu.get_barrier_semaphore()
    for to in (to_xp, to_xm, to_xo, to_yp, to_ym):
        pl.semaphore_signal(barrier, inc=1, device_id=to, device_id_type=MESH)
    for dz, dc in z_peers:
        pl.semaphore_signal(barrier, inc=1, device_id=z_peer(dz, dc), device_id_type=MESH)
    pl.semaphore_wait(barrier, 5 + len(z_peers))

    def start(sx):
        return (21 * sx + lax.div(sx, 2)) * 128

    def bcols(sx, j):
        return pl.ds(pl.multiple_of(start(sx) + CH[j][0], 128), CH[j][1])

    def cols(j):
        return slice(CH[j][0], CH[j][0] + CH[j][1])

    def krows(sx, sy, off=0, n=KB):
        return pl.ds(pl.multiple_of((sx * Y + sy) * KB + off, 64), n)

    def arows(sx):
        return pl.ds(pl.multiple_of(sx * RB, RB), RB)

    own_b = b_ref.at[:, pl.ds(pl.multiple_of(start(x), 128), NS)]
    own_dst = bf.at[krows(x, y), :]
    def y_own():
        send(own_b, own_dst, s_yo, yo.at[0], to_yp)
        send(own_b, own_dst, s_yo, yo.at[1], to_ym)
        pltpu.make_async_copy(own_b, own_dst, loc.at[0]).start()

    def y_own_forward():
        take(own_dst, yo.at[0])
        blk = bf.at[krows(x, ym, 0, 64), :]
        send(blk, blk, s_yo, yow.at[0], to_yp)
        take(own_dst, yo.at[1])
        blk = bf.at[krows(x, yp, 64, 64), :]
        send(blk, blk, s_yo, yow.at[1], to_ym)

    def x_send(j):
        for i, (sx, to) in enumerate(x_peers):
            send(b_ref.at[:, bcols(sx, j)], bf.at[krows(x, y), cols(j)], s_x, xd.at[i, j], to)

    def y_direct(j):
        for i, sx in enumerate((xm, xp, xo)):
            blk = bf.at[krows(sx, y), cols(j)]
            take(blk, xd.at[i, j])
            send(blk, blk, s_y, yd.at[0, j], to_yp)
            send(blk, blk, s_y, yd.at[1, j], to_ym)

    def y_forward(j):
        take(bf.at[0:3 * KB, cols(j)], yd.at[0, j])
        for sx in (xm, xp, xo):
            blk = bf.at[krows(sx, ym, 0, 64), cols(j)]
            send(blk, blk, s_y, yf.at[0, j], to_yp)
        take(bf.at[0:3 * KB, cols(j)], yd.at[1, j])
        for sx in (xm, xp, xo):
            blk = bf.at[krows(sx, yp, 64, 64), cols(j)]
            send(blk, blk, s_y, yf.at[1, j], to_ym)

    def a_seg(sx, sc, sz):
        return a_ref.at[:, pl.ds(pl.multiple_of(((sx * 2 + sc) * Z * Y + sz * Y) * KB, Y * KB), Y * KB)]

    def a_send():
        for dz, dc in z_peers:
            pos, pc = REL.index((Z - dz) % Z), lax.rem(c + dc, 2)
            for sx in range(X):
                dst = af.at[pos, c, arows(x), sx * Y * KB:(sx + 1) * Y * KB]
                send(a_seg(sx, pc, ahead(dz)), dst, s_az, az.at[pos, c], z_peer(dz, dc))
        for sx in range(X):
            dst = af.at[Z - 1, c, arows(x), sx * Y * KB:(sx + 1) * Y * KB]
            pltpu.make_async_copy(a_seg(sx, c, z), dst, loc.at[1]).start()

    def a_direct(g):
        lo, hi = GROUPS[g]
        for pos in range(lo, hi):
            for sc in (c, cc):
                own = REL[pos] == 0 and sc is c
                take(af.at[pos, sc, arows(x), :], loc.at[1] if own else az.at[pos, sc])
        blk = af.at[lo:hi, :, arows(x), :]
        send(blk, blk, s_ax, ax.at[0, g], to_xp)
        send(blk, blk, s_ax, ax.at[1, g], to_xm)

    def a_forward(g):
        lo, hi = GROUPS[g]
        take(af.at[lo:hi, :, arows(xm), :], ax.at[0, g])
        blk = af.at[lo:hi, :, arows(xm), 0:K // 2]
        send(blk, blk, s_ax, aw.at[0, g], to_xp)
        take(af.at[lo:hi, :, arows(xp), :], ax.at[1, g])
        blk = af.at[lo:hi, :, arows(xp), K // 2:K]
        send(blk, blk, s_ax, aw.at[1, g], to_xm)

    done = set()

    def once(key, fn):
        if key not in done:
            done.add(key)
            fn()

    def b_whole():
        take(own_dst, loc.at[0])
        for d in range(2):
            take(bf.at[0:64, :], yow.at[d])

    def b_chunk(j):
        for d in range(2):
            take(bf.at[0:3 * 64, cols(j)], yf.at[d, j])

    def a_group(g):
        lo, hi = GROUPS[g]
        take(af.at[lo:hi, :, arows(xo), 0:K // 2], aw.at[0, g])
        take(af.at[lo:hi, :, arows(xo), K // 2:K], aw.at[1, g])

    def dot(pos, n, j):
        lhs = af[pl.ds(pos, n)].reshape(n * 2 * BLK, K)
        out = jnp.dot(lhs, bf[:, cols(j)], preferred_element_type=jnp.float32)
        part[pl.ds(pos, n), :, :, cols(j)] = out.reshape(n, 2, BLK, CH[j][1])

    def matmul(j, g):
        once("b", b_whole)
        once(("b", j), lambda: b_chunk(j))
        lo, hi = (0, Z) if g < 0 else GROUPS[g]
        for k in range(5) if g < 0 else (g,):
            once(("a", k), lambda: a_group(k))
        if g < 0:
            @pl.loop(0, Z // 2)
            def _(m):
                dot(m * 2, 2, j)
        else:
            dot(lo, hi - lo, j)
        send(part.at[lo:hi, cc, :, cols(j)], rcv.at[lo:hi, :, cols(j)], s_c, cr.at[max(g, 0), j], to_core)

    def core_take(j, g):
        if j < PHASED:
            lo, hi = GROUPS[g]
            take(rcv.at[lo:hi, :, cols(j)], cr.at[g, j])
        elif g == 0:
            take(rcv.at[:, :, cols(j)], cr.at[0, j])

    HR = (slice(0, BLK // 2), slice(BLK // 2, BLK))

    def z_step(j, s):
        core_take(j, s)
        if s == 0:
            part[0, c, :, cols(j)] += rcv[0, :, cols(j)]
            for d, to in enumerate((to_zp, to_zm)):
                send(part.at[0, c, HR[d], cols(j)], zr.at[d, 0, HR[d], cols(j)], s_c, zs.at[4 * d, j], to)
            return
        for d, to in enumerate((to_zp, to_zm)):
            pos = 2 * s - 1 + d
            if s == 1:
                take(zr.at[d, 0, HR[d], cols(j)], zs.at[4 * d, j])
                part[pos, c, HR[d], cols(j)] += rcv[pos, HR[d], cols(j)] + zr[d, 0, HR[d], cols(j)]
                part[pos, c, HR[1 - d], cols(j)] += rcv[pos, HR[1 - d], cols(j)]
            else:
                take(zr.at[d, s - 1, :, cols(j)], zs.at[4 * d + s - 1, j])
                part[pos, c, :, cols(j)] += rcv[pos, :, cols(j)] + zr[d, s - 1, :, cols(j)]
            send(part.at[pos, c, :, cols(j)], zr.at[d, s, :, cols(j)], s_c, zs.at[4 * d + s, j], to)

    def finish(j):
        core_take(j, 4)
        for d in range(2):
            take(zr.at[d, 3, :, cols(j)], zs.at[4 * d + 3, j])
        total = part[7, c, :, cols(j)] + rcv[7, :, cols(j)] + zr[0, 3, :, cols(j)] + zr[1, 3, :, cols(j)]
        cs[:, cols(j)] = total.astype(jnp.bfloat16)

        def out():
            dst = o_ref.at[:, bcols(x, j)]
            for sx, to in x_peers:
                rows = pl.ds(pl.multiple_of(sx * RB, RB), RB)
                send(cs.at[rows, cols(j)], dst, s_o, cx.at[j], to)
            rows = pl.ds(pl.multiple_of(x * RB, RB), RB)
            pltpu.make_async_copy(cs.at[rows, cols(j)], dst, loc.at[2]).start()

        if j == 0:
            pl.when(lax.rem(x, 2) == 0)(out)
        else:
            out()

    run = {"yo": y_own, "yfo": y_own_forward, "x": x_send, "yd": y_direct, "yf": y_forward,
           "as": a_send, "ad": a_direct, "af": a_forward, "mm": matmul, "z": z_step,
           "fin": finish}
    for op in ORDER:
        run[op[0]](*op[1:])

    even = lax.rem(x, 2) == 0
    w0 = CH[0][1]
    for j in range(1, NCH):
        take(bf.at[0:3 * RB, cols(j)], cx.at[j])

    @pl.when(even)
    def _():
        take(bf.at[0:RB, 0:w0], cx.at[0])
        take(bf.at[0:RB, :], loc.at[2])
        take(bf.at[0:3 * RB, :], s_o)

    @pl.when(jnp.logical_not(even))
    def _():
        take(bf.at[0:2 * RB, 0:w0], cx.at[0])
        take(bf.at[0:RB, w0:], loc.at[2])
        take(bf.at[0:3 * RB, w0:], s_o)

    take(bf.at[0:3 * KB, :], s_x)
    take(bf.at[0:9 * KB, :], s_y)
    take(bf.at[0:3 * KB, :], s_yo)
    take(bf.at[0:1920, :], s_c)
    take(af.at[0:5, 0, 0:48, :], s_az)
    take(af.at[0:6], s_ax)


def solution(mesh):
    spec_rows = P(("dp", "tp"), None)
    dma = pltpu.SemaphoreType.DMA

    call = pl.pallas_call(
        kernel,
        out_shape=jax.ShapeDtypeStruct((RB, 11008), jnp.bfloat16),
        in_specs=[pl.BlockSpec(memory_space=pl.ANY)] * 2,
        out_specs=pl.BlockSpec(memory_space=pl.ANY),
        scratch_shapes=[
            pltpu.VMEM((Z, 2, BLK, K), jnp.bfloat16),
            pltpu.VMEM((K, NS), jnp.bfloat16),
            pltpu.VMEM((Z, 2, BLK, NS), jnp.float32),
            pltpu.VMEM((Z, BLK, NS), jnp.float32),
            pltpu.VMEM((2, 4, BLK, NS), jnp.float32),
            pltpu.VMEM((BLK, NS), jnp.bfloat16),
            dma((Z, 2)), dma((2, 5)), dma((2, 5)), dma((2,)), dma((2,)),
            dma((3, NCH)), dma((2, NCH)), dma((2, NCH)),
            dma((5, NCH)), dma((8, NCH)), dma((NCH,)), dma((3,)),
            dma, dma, dma, dma, dma, dma, dma,
        ],
        compiler_params=pltpu.CompilerParams(
            collective_id=0, has_side_effects=True, vmem_limit_bytes=60 * 1024 * 1024),
    )

    return jax.shard_map(call, mesh=mesh, in_specs=(spec_rows, spec_rows), out_specs=spec_rows, check_vma=False)
```

time: 662 us -> 133 us (0.20)
  waiting for transfers between devices: 591 us -> 0 us
  Pallas kernels: 0 us -> 131 us
  matrix products: 32.7 us -> 0 us
  blocking collectives: 20.5 us -> 0 us
  between operations: 13.4 us -> 0.01 us
    all_gather x1 -> x0, waiting for transfers between devices: 551 us -> none  [local_block(): b_slab = lax.all_gather(b_rows, 'tp', axis=0, tiled=True)]
    pallas_call x0 -> x1, Pallas kernels: none -> 131 us
    reduce_scatter x1 -> x0, waiting for transfers between devices: 39.5 us -> none  [local_block(): summed = lax.psum_scatter(part_prod, 'dp', scatter_dimension=0, tiled=True)]
    dot_general x1 -> x0, matrix products: 32.7 us -> none  [local_block(): part_prod = jnp.dot(a_cols, b_slab, preferred_element_type=jnp.float32)]
    all_to_all x1 -> x0, blocking collectives: 20.5 us -> none  [local_block(): a_cols = lax.all_to_all(a_rows, 'dp', 1, 0, tiled=True)]
  transfers between devices with their start and end apart: 2 -> 0, of which waited for: 2 -> 0; matrix products, arithmetic and copies ran while one was open for 0% -> 0% of each run, Pallas kernels for 0% -> 0%
where the time goes in v2:
time: 133 us
  Pallas kernels  131 us (98%)
  local copies, waits for them, and re-layouts  1.74 us (1%)
    pallas_call x1, Pallas kernels  131 us

profile of v2, /device:TPU:1, one launch (start us, length us, event | category | flops | bytes accessed | tf_op | source)
XLA Modules:
  0.0 132.6 jit_solution(2454796998077688604)
XLA Ops:
  0.0 130.9 %shard_map.28 = bf16[16,11008]{1,0:T(8,128)(2,1)} custom-call(bf16[16,32768]{1,0:T(8,128)(2,1)} %a_ref.1, bf16[128,11008]{1,0:T(8,128)(2,1)} %b_ref.1), custom_call_target="tpu_custom_call" | custom-call | tf_op jit(solution)/shard_map/pallas_call
  130.9 1.7 %copy.4 = bf16[16,11008]{1,0:T(8,128)(2,1)} copy(bf16[16,11008]{1,0:T(8,128)(2,1)} %shard_map.28) | data formatting | bytes 704512

commit v3 on v2

--- a/solution.py
+++ b/solution.py
@@ -14,38 +14,41 @@
 NS = 22 * 128
 BLK = X * RB
 
-WIDTHS = [128] + [256] * 10 + [128]
+WIDTHS = [128, 384, 384, 384, 256, 256, 256, 256, 256, 128, 128]
 CH = [(sum(WIDTHS[:j]), w) for j, w in enumerate(WIDTHS)]
 NCH = len(CH)
 
 REL = (4, 3, 5, 2, 6, 1, 7, 0)
 GROUPS = ((0, 1), (1, 3), (3, 5), (5, 7), (7, 8))
-PHASED = 6
+DIRECT = 99
+PHASED = 11
 
 ORDER = (
-    ("yo",), ("x", 0), ("as",), ("x", 1), ("x", 2), ("ad", 0), ("yd", 0), ("yd", 1), ("x", 3), ("af", 0),
-    ("yfo",), ("ad", 1), ("yf", 0), ("x", 4), ("ad", 2), ("yf", 1), ("x", 5), ("yd", 2), ("af", 1), ("mm", 0, 0),
-    ("yd", 3), ("z", 0, 0), ("x", 6), ("mm", 1, 0), ("z", 1, 0), ("af", 2), ("yd", 4), ("yf", 2), ("ad", 3),
-    ("mm", 0, 1), ("mm", 1, 1), ("yf", 3), ("z", 0, 1), ("z", 1, 1), ("x", 7), ("yd", 5), ("mm", 0, 2),
-    ("yf", 4), ("mm", 1, 2), ("x", 8), ("z", 0, 2), ("mm", 2, 2), ("z", 1, 2), ("mm", 2, 1), ("mm", 2, 0),
-    ("ad", 4), ("mm", 3, 2), ("mm", 3, 1), ("yd", 6), ("z", 2, 0), ("mm", 3, 0), ("x", 9), ("z", 3, 0),
-    ("yf", 5), ("z", 2, 1), ("af", 3), ("mm", 4, 2), ("z", 3, 1), ("mm", 4, 1), ("yd", 7), ("mm", 4, 0),
-    ("x", 10), ("z", 2, 2), ("z", 4, 0), ("yf", 6), ("z", 3, 2), ("af", 4), ("mm", 5, 2), ("mm", 5, 1),
-    ("yd", 8), ("z", 4, 1), ("mm", 5, 0), ("x", 11), ("mm", 0, 3), ("mm", 1, 3), ("z", 5, 0), ("mm", 2, 3),
-    ("yf", 7), ("z", 0, 3), ("mm", 3, 3), ("z", 1, 3), ("z", 4, 2), ("z", 2, 3), ("mm", 4, 3), ("mm", 5, 3),
-    ("z", 3, 3), ("yd", 9), ("z", 5, 1), ("mm", 0, 4), ("mm", 1, 4), ("mm", 2, 4), ("mm", 3, 4), ("mm", 4, 4),
-    ("mm", 5, 4), ("fin", 0), ("fin", 1), ("mm", 6, -1), ("yf", 8), ("z", 4, 3), ("fin", 2), ("mm", 7, -1),
-    ("yd", 10), ("fin", 3), ("z", 6, 0), ("z", 5, 2), ("z", 7, 0), ("fin", 4), ("yf", 9), ("z", 6, 1),
-    ("mm", 8, -1), ("yd", 11), ("z", 5, 3), ("z", 7, 1), ("z", 6, 2), ("z", 8, 0), ("yf", 10), ("fin", 5),
-    ("mm", 9, -1), ("z", 7, 2), ("yf", 11), ("z", 6, 3), ("z", 8, 1), ("z", 9, 0), ("mm", 10, -1), ("z", 7, 3),
-    ("mm", 11, -1), ("fin", 6), ("z", 10, 0), ("z", 8, 2), ("z", 11, 0), ("z", 9, 1), ("fin", 7), ("z", 10, 1),
-    ("z", 8, 3), ("z", 11, 1), ("z", 9, 2), ("z", 10, 2), ("fin", 8), ("z", 11, 2), ("z", 9, 3), ("z", 10, 3),
-    ("z", 11, 3), ("fin", 9), ("fin", 10), ("fin", 11),
+    ("yo",), ("x", 3), ("in",), ("x", 2), ("x", 1), ("as", 0), ("as", 1), ("as", 2), ("as", 3), ("yd", 2),
+    ("x", 0), ("x", 9), ("ad", 0), ("x", 5), ("yfo",), ("af", 0), ("ad", 1), ("as", 4), ("yd", 1), ("yf", 2),
+    ("ad", 2), ("ad", 3), ("af", 1), ("yd", 3), ("mm", 2, 0), ("yf", 1), ("af", 2), ("yd", 9), ("ad", 4),
+    ("z", 2, 0), ("mm", 2, 1), ("z", 2, 1), ("yf", 3), ("af", 3), ("x", 8), ("af", 4), ("yd", 5), ("yd", 0),
+    ("mm", 1, 0), ("mm", 2, 2), ("x", 6), ("z", 1, 0), ("x", 4), ("mm", 1, 2), ("z", 2, 2), ("mm", 1, 1),
+    ("mm", 3, 0), ("mm", 2, 3), ("z", 1, 1), ("x", 7), ("z", 3, 0), ("yf", 9), ("mm", 1, 3), ("mm", 3, 1),
+    ("mm", 3, 4), ("yf", 5), ("z", 2, 3), ("mm", 2, 4), ("z", 1, 2), ("yd", 6), ("mm", 9, 0), ("yd", 4),
+    ("z", 3, 1), ("mm", 3, 3), ("fin", 2), ("mm", 9, 2), ("mm", 5, 2), ("yf", 0), ("z", 9, 0), ("mm", 5, 0),
+    ("z", 1, 3), ("mm", 3, 2), ("z", 5, 0), ("mm", 9, 4), ("x", 10), ("mm", 1, 4), ("z", 3, 2), ("yf", 6),
+    ("mm", 5, 1), ("mm", 9, 1), ("fin", 1), ("z", 9, 1), ("z", 5, 1), ("mm", 9, 3), ("yf", 4), ("yd", 8),
+    ("mm", 5, 4), ("mm", 5, 3), ("mm", 0, 0), ("z", 3, 3), ("mm", 6, 0), ("z", 9, 2), ("z", 5, 2), ("mm", 6, 1),
+    ("mm", 6, 2), ("mm", 4, 0), ("z", 6, 0), ("mm", 4, 2), ("fin", 3), ("yd", 7), ("mm", 6, 4), ("z", 9, 3),
+    ("z", 4, 0), ("mm", 4, 1), ("mm", 0, 2), ("z", 5, 3), ("yf", 8), ("mm", 0, 1), ("z", 6, 1), ("fin", 9),
+    ("mm", 6, 3), ("mm", 0, 4), ("z", 0, 0), ("z", 4, 1), ("yd", 10), ("fin", 5), ("mm", 4, 3), ("z", 6, 2),
+    ("mm", 0, 3), ("z", 0, 1), ("yf", 7), ("mm", 8, 0), ("mm", 4, 4), ("z", 4, 2), ("yf", 10), ("z", 6, 3),
+    ("z", 0, 2), ("z", 8, 0), ("mm", 8, 2), ("mm", 7, 0), ("mm", 7, 1), ("mm", 8, 1), ("mm", 10, 0), ("z", 7, 0),
+    ("mm", 10, 2), ("z", 4, 3), ("fin", 6), ("z", 10, 0), ("mm", 7, 3), ("z", 8, 1), ("z", 7, 1), ("mm", 10, 1),
+    ("z", 0, 3), ("fin", 4), ("mm", 10, 4), ("mm", 7, 2), ("z", 10, 1), ("z", 8, 2), ("mm", 8, 3), ("z", 7, 2),
+    ("fin", 0), ("mm", 7, 4), ("z", 10, 2), ("z", 8, 3), ("mm", 10, 3), ("mm", 8, 4), ("z", 7, 3), ("z", 10, 3),
+    ("fin", 8), ("fin", 7), ("fin", 10),
 )
 
 
 def kernel(a_ref, b_ref, o_ref, af, bf, part, rcv, zr, cs,
-           az, ax, aw, yo, yow, xd, yd, yf, cr, zs, cx, loc,
+           az, ax, aw, yo, yow, xd, yd, yf, cr, zs, cx, loc, late,
            s_x, s_y, s_yo, s_az, s_ax, s_c, s_o):
     dp, tp = lax.axis_index("dp"), lax.axis_index("tp")
     x, c = lax.div(dp, 2), lax.rem(dp, 2)
@@ -79,12 +82,21 @@
     def z_peer(dz, dc):
         return dev(x, y, ahead(dz), lax.rem(c + dc, 2))
 
+    level = c * Z + z
     barrier = pltpu.get_barrier_semaphore()
     for to in (to_xp, to_xm, to_xo, to_yp, to_ym):
         pl.semaphore_signal(barrier, inc=1, device_id=to, device_id_type=MESH)
-    for dz, dc in z_peers:
-        pl.semaphore_signal(barrier, inc=1, device_id=z_peer(dz, dc), device_id_type=MESH)
-    pl.semaphore_wait(barrier, 5 + len(z_peers))
+
+    def tell_z(sem, below):
+        for dz, dc in z_peers:
+            theirs = lax.rem(c + dc, 2) * Z + ahead(dz)
+
+            @pl.when(theirs < level if below else level < theirs)
+            def _():
+                pl.semaphore_signal(sem, inc=1, device_id=z_peer(dz, dc), device_id_type=MESH)
+
+    tell_z(barrier, False)
+    pl.semaphore_wait(barrier, 5 + level)
 
     def start(sx):
         return (21 * sx + lax.div(sx, 2)) * 128
@@ -140,15 +152,31 @@
     def a_seg(sx, sc, sz):
         return a_ref.at[:, pl.ds(pl.multiple_of(((sx * 2 + sc) * Z * Y + sz * Y) * KB, Y * KB), Y * KB)]
 
-    def a_send():
+    done = set()
+
+    def once(key, fn):
+        if key not in done:
+            done.add(key)
+            fn()
+
+    def late_wait():
+        @pl.when(level < len(z_peers))
+        def _():
+            pl.semaphore_wait(late, len(z_peers) - level)
+
+    def a_send(g):
+        once("late", late_wait)
+        lo, hi = GROUPS[g]
         for dz, dc in z_peers:
             pos, pc = REL.index((Z - dz) % Z), lax.rem(c + dc, 2)
+            if lo <= pos < hi:
+                for sx in range(X):
+                    dst = af.at[pos, c, arows(x), sx * Y * KB:(sx + 1) * Y * KB]
+                    send(a_seg(sx, pc, ahead(dz)), dst, s_az, az.at[pos, c], z_peer(dz, dc))
+        if hi == Z:
             for sx in range(X):
-                dst = af.at[pos, c, arows(x), sx * Y * KB:(sx + 1) * Y * KB]
-                send(a_seg(sx, pc, ahead(dz)), dst, s_az, az.at[pos, c], z_peer(dz, dc))
-        for sx in range(X):
-            dst = af.at[Z - 1, c, arows(x), sx * Y * KB:(sx + 1) * Y * KB]
-            pltpu.make_async_copy(a_seg(sx, c, z), dst, loc.at[1]).start()
+                dst = af.at[Z - 1, c, arows(x), sx * Y * KB:(sx + 1) * Y * KB]
+                pltpu.make_async_copy(a_seg(sx, c, z), dst, loc.at[1]).start()
 
     def a_direct(g):
         lo, hi = GROUPS[g]
@@ -168,13 +196,6 @@
         take(af.at[lo:hi, :, arows(xp), :], ax.at[1, g])
         blk = af.at[lo:hi, :, arows(xp), K // 2:K]
         send(blk, blk, s_ax, aw.at[1, g], to_xm)
-
-    done = set()
-
-    def once(key, fn):
-        if key not in done:
-            done.add(key)
-            fn()
 
     def b_whole():
         take(own_dst, loc.at[0])
@@ -220,6 +241,12 @@
 
     def z_step(j, s):
         core_take(j, s)
+        if j >= DIRECT:
+            for pos in range(Z - 1):
+                part[pos, c, :, cols(j)] += rcv[pos, :, cols(j)]
+                send(part.at[pos, c, :, cols(j)], zr.at[pos // 4, pos % 4, :, cols(j)], s_c, zs.at[pos, j],
+                     dev(x, y, ahead(REL[pos]), c))
+            return
         if s == 0:
             part[0, c, :, cols(j)] += rcv[0, :, cols(j)]
             for d, to in enumerate((to_zp, to_zm)):
@@ -238,9 +265,11 @@
 
     def finish(j):
         core_take(j, 4)
-        for d in range(2):
-            take(zr.at[d, 3, :, cols(j)], zs.at[4 * d + 3, j])
-        total = part[7, c, :, cols(j)] + rcv[7, :, cols(j)] + zr[0, 3, :, cols(j)] + zr[1, 3, :, cols(j)]
+        total = part[7, c, :, cols(j)] + rcv[7, :, cols(j)]
+        for slot in range(7) if j >= DIRECT else (3, 7):
+            got = zr.at[slot // 4, slot % 4, :, cols(j)]
+            take(got, zs.at[slot, j])
+            total = total + got[...]
         cs[:, cols(j)] = total.astype(jnp.bfloat16)
 
         def out():
@@ -256,9 +285,11 @@
         else:
             out()
 
-    run = {"yo": y_own, "yfo": y_own_forward, "x": x_send, "yd": y_direct, "yf": y_forward,
-           "as": a_send, "ad": a_direct, "af": a_forward, "mm": matmul, "z": z_step,
-           "fin": finish}
+    def reply():
+        tell_z(late, True)
+
+    run = {"in": reply, "yo": y_own, "yfo": y_own_forward, "x": x_send, "yd": y_direct, "yf": y_forward,
+           "as": a_send, "ad": a_direct, "af": a_forward, "mm": matmul, "z": z_step, "fin": finish}
     for op in ORDER:
         run[op[0]](*op[1:])
 
@@ -305,7 +336,7 @@
             pltpu.VMEM((BLK, NS), jnp.bfloat16),
             dma((Z, 2)), dma((2, 5)), dma((2, 5)), dma((2,)), dma((2,)),
             dma((3, NCH)), dma((2, NCH)), dma((2, NCH)),
-            dma((5, NCH)), dma((8, NCH)), dma((NCH,)), dma((3,)),
+            dma((5, NCH)), dma((8, NCH)), dma((NCH,)), dma((3,)), pltpu.SemaphoreType.REGULAR,
             dma, dma, dma, dma, dma, dma, dma,
         ],
         compiler_params=pltpu.CompilerParams(

time: 133 us -> 130 us (0.977)
  Pallas kernels: 131 us -> 128 us
    pallas_call x1, Pallas kernels: 131 us -> 128 us
where the time goes in v3:
time: 130 us
  Pallas kernels  128 us (98%)
  local copies, waits for them, and re-layouts  1.74 us (1%)
    pallas_call x1, Pallas kernels  128 us

profile of v3, /device:TPU:1, one launch (start us, length us, event | category | flops | bytes accessed | tf_op | source)
XLA Modules:
  0.0 129.8 jit_solution(8349369686027715111)
XLA Ops:
  0.0 128.0 %shard_map.28 = bf16[16,11008]{1,0:T(8,128)(2,1)} custom-call(bf16[16,32768]{1,0:T(8,128)(2,1)} %a_ref.1, bf16[128,11008]{1,0:T(8,128)(2,1)} %b_ref.1), custom_call_target="tpu_custom_call" | custom-call | tf_op jit(solution)/shard_map/pallas_call
  128.0 1.7 %copy.4 = bf16[16,11008]{1,0:T(8,128)(2,1)} copy(bf16[16,11008]{1,0:T(8,128)(2,1)} %shard_map.28) | data formatting | bytes 704512

commit v4 on v3

--- a/solution.py
+++ b/solution.py
@@ -24,7 +24,7 @@
 PHASED = 11
 
 ORDER = (
-    ("yo",), ("x", 3), ("in",), ("x", 2), ("x", 1), ("as", 0), ("as", 1), ("as", 2), ("as", 3), ("yd", 2),
+    ("in",), ("yo",), ("x", 3), ("x", 2), ("x", 1), ("as", 0), ("as", 1), ("as", 2), ("as", 3), ("yd", 2),
     ("x", 0), ("x", 9), ("ad", 0), ("x", 5), ("yfo",), ("af", 0), ("ad", 1), ("as", 4), ("yd", 1), ("yf", 2),
     ("ad", 2), ("ad", 3), ("af", 1), ("yd", 3), ("mm", 2, 0), ("yf", 1), ("af", 2), ("yd", 9), ("ad", 4),
     ("z", 2, 0), ("mm", 2, 1), ("z", 2, 1), ("yf", 3), ("af", 3), ("x", 8), ("af", 4), ("yd", 5), ("yd", 0),
@@ -274,7 +274,7 @@
 
         def out():
             dst = o_ref.at[:, bcols(x, j)]
-            for sx, to in x_peers:
+            for sx, to in x_peers[::-1]:
                 rows = pl.ds(pl.multiple_of(sx * RB, RB), RB)
                 send(cs.at[rows, cols(j)], dst, s_o, cx.at[j], to)
             rows = pl.ds(pl.multiple_of(x * RB, RB), RB)

time: 130 us -> 130 us (level)
  no operation moved by 1% of the time
where the time goes in v4:
time: 130 us
  Pallas kernels  128 us (98%)
  local copies, waits for them, and re-layouts  1.74 us (1%)
    pallas_call x1, Pallas kernels  128 us

profile of v4, /device:TPU:1, one launch (start us, length us, event | category | flops | bytes accessed | tf_op | source)
XLA Modules:
  0.0 129.7 jit_solution(2929251365445498580)
XLA Ops:
  0.0 127.9 %shard_map.28 = bf16[16,11008]{1,0:T(8,128)(2,1)} custom-call(bf16[16,32768]{1,0:T(8,128)(2,1)} %a_ref.1, bf16[128,11008]{1,0:T(8,128)(2,1)} %b_ref.1), custom_call_target="tpu_custom_call" | custom-call | tf_op jit(solution)/shard_map/pallas_call
  127.9 1.7 %copy.4 = bf16[16,11008]{1,0:T(8,128)(2,1)} copy(bf16[16,11008]{1,0:T(8,128)(2,1)} %shard_map.28) | data formatting | bytes 704512
